TPU v7x, 128 devices: a whole 4x4x4 slice. The times are simulated.
128 devices in a mesh: grp: 4 (over z_lo, core), blk: 32 (over x, z_hi, y).
Axes of the slice: x: 4, y: 4, z: 4 (z_hi: 2, z_lo: 2; z = z_hi * 2 + z_lo), core: 2. Of those that a mesh axis runs over, the one named last changes fastest.
Arguments:
- residual: float32 [3, 64, 128, 512], P(None, 'blk', None, 'grp'), may hold values from -8 to 8
- face_mask: int32 [3, 64, 128, 512], P(None, 'blk', None, 'grp'), may hold values 0 or 1
- conductivity: float32 [4, 64, 128, 512], P('grp', 'blk'), may hold values from 0.5 to 4
- stencil: float32 [4, 27, 3, 3], replicated, may hold values from -1.5 to 1.5, as said below
Outputs:
- correction: float32 [3, 64, 128, 512], P(None, 'blk', None, 'grp')
Inputs may be any that keep to these rules, and one draw needn't show every extreme that they name: In each space's stencil the diagonal of the block at offset 0 exceeds the sum of magnitudes of all other entries of its row.
All inputs are finite; a program needn't handle non-finite values. No bound on the sum of `face_mask` on one device may be relied on, other than what follows from the above.
Results may differ from a plain program's by a relative error of at most 0.0001.
Values sent between devices are 32-bit elements; how exact they have to be, the bound alone decides.
No kernel may reach another device: no remote copies, remote signals or barrier semaphores. Data moves between devices by JAX's collectives and lax.ppermute only.
A program may use at most 192 MiB of HBM per device.

v0:
```python
import jax
import jax.numpy as jnp
from jax import lax
from jax.experimental import pallas as pl
from jax.experimental.pallas import tpu as pltpu
from jax.sharding import PartitionSpec as P

OMEGA = 0.8
F32 = jnp.float32
BF16 = jnp.bfloat16
N = 128
INV = 136
PLANES = 32
MROWS = 144
HROWS = 136
WROWS = 136
BLOCK = 6
PAIRS = 11
TERM = 48
DEPTH = 3 * TERM


def vmem():
    return pl.BlockSpec(memory_space=pltpu.VMEM)


def smem():
    return pl.BlockSpec(memory_space=pltpu.SMEM)


def call(kernel, out_shapes, in_specs, scratch=(), dtype=F32, outs=None):
    return pl.pallas_call(
        kernel,
        out_shape=[jax.ShapeDtypeStruct(shape, dtype) for shape in out_shapes],
        in_specs=in_specs,
        out_specs=[outs or vmem() for _ in out_shapes],
        scratch_shapes=list(scratch),
        compiler_params=pltpu.CompilerParams(vmem_limit_bytes=50 << 20),
    )


def from_below(v):
    lane = lax.broadcasted_iota(jnp.int32, v.shape, 1)
    return jnp.where(lane == 0, 0.0, pltpu.roll(v, 1, 1))


def from_above(v):
    lane = lax.broadcasted_iota(jnp.int32, v.shape, 1)
    return jnp.where(lane == N - 1, 0.0, pltpu.roll(v, N - 1, 1))


def mask_residual(
    place, res_hbm, mask_hbm, cond_hbm, own, first, second, cond, res, mask, sems
):
    odd = place[1] % 2
    copies = [
        pltpu.make_async_copy(src, dst, sems.at[i])
        for i, (src, dst) in enumerate(((res_hbm, res), (mask_hbm, mask), (cond_hbm, cond)))
    ]
    for copy in copies:
        copy.start()
    copies[0].wait()
    copies[1].wait()
    for comp in range(3):
        for layer in range(2):
            own[comp, layer] = (res[comp, layer] * mask[comp, layer].astype(F32)).T
    for slot in range(2):
        first[slot] = own[slot + 1, odd]
        second[slot] = own[slot + 1, 1 - odd]
    copies[2].wait()


def invert(cond, chunks):
    for layer in range(2):
        base = layer * INV
        chunks[0, base : base + 2] = jnp.zeros((2, N), F32)
        chunks[3, base + 130 : base + 132] = jnp.zeros((2, N), F32)
        for j in range(4):
            v = (1.0 / cond[0, layer, :, j * N : (j + 1) * N]).T
            chunks[j, base + 2 : base + 130] = v
            chunks[j, base + 132 : base + INV] = jnp.zeros((4, N), F32)
            if j < 3:
                chunks[j + 1, base : base + 2] = v[N - 2 : N]
            if j > 0:
                chunks[j - 1, base + 130 : base + 132] = v[0:2]


def plane_row(comp, layer):
    if layer in (0, 1):
        return (comp * 2 + layer) * 3
    return 18 + ((comp - 1) * 2 + max(layer, 0) // 2) * 3


def pack(place, own, x_first, x_second, first, second, planes):
    z_odd = place[0] % 2
    odd = place[1] % 2

    def put(row, v):
        planes[0, row : row + 3] = v[0:3]
        planes[1, row : row + 3] = v[N - 3 : N]

    for comp in range(3):
        for layer in range(2):
            put(plane_row(comp, layer), own.at[comp, layer])
    for slot in range(2):
        low_row = plane_row(slot + 1, -1)
        for arrived, upper in ((x_first, odd), (x_second, 1 - odd)):
            row = low_row + 3 * upper
            v = arrived.at[slot]
            planes[0, pl.ds(row, 3)] = v[0:3]
            planes[1, pl.ds(row, 3)] = v[N - 3 : N]
    planes[:, 30:PLANES] = jnp.zeros((2, PLANES - 30, N), F32)
    first[...] = planes[z_odd]
    second[...] = planes[1 - z_odd]


def fill_masked(place, own, x_first, x_second, z_first, z_second, field, side, planes):
    z_odd = place[0] % 2
    odd = place[1] % 2
    planes[0] = z_first[...]
    planes[1] = z_second[...]
    for arrived, where in ((x_first, odd), (x_second, 1 - odd)):
        for slot in range(2):
            side[where, slot, 3 : 3 + N] = arrived[slot]

    def ends(ref, row):
        ref[0:3] = planes[z_odd, row : row + 3]
        ref[3 + N : 6 + N] = planes[1 - z_odd, row : row + 3]
        ref[6 + N : MROWS] = jnp.zeros((MROWS - N - 6, N), F32)

    for layer in range(2):
        for comp in range(3):
            field[layer, comp, 3 : 3 + N] = own[comp, layer]
            ends(field.at[layer, comp], plane_row(comp, layer))
    for where, layer in ((0, -1), (1, 2)):
        for slot in range(2):
            ends(side.at[where, slot], plane_row(slot + 1, layer))


def restrict_tile(field, side, place, start, rows):
    def at(layer, comp, shift):
        rows_at = slice(start + 1 + shift, start + 1 + shift + rows)
        if layer in (1, 2):
            return field[layer - 1, comp, rows_at]
        return side[layer // 3, comp - 1, rows_at]

    x0, xm, xp = (at(place, 0, s) for s in (0, -1, 1))
    y0, ym, yp = (at(place, 1, s) for s in (0, -1, 1))
    z0 = at(place, 2, 0)
    yl0, ylm, ylp = (at(place - 1, 1, s) for s in (0, -1, 1))
    zl0 = at(place - 1, 2, 0)
    yn0, ynm = (at(place + 1, 1, s) for s in (0, -1))
    zn0 = at(place + 1, 2, 0)
    xsum = x0 + xm
    zsum = z0 + zl0
    curl_x = z0 - from_below(z0) - y0 + ym
    curl_x_next = zn0 - from_below(zn0) - yn0 + ynm
    curl_y = x0 - xm - z0 + zl0
    curl_z = y0 - yl0 - x0 + from_below(x0)
    curl_z_next = yp - ylp - xp + from_below(xp)
    return (
        (x0, y0, z0),
        (
            0.25 * (xsum + from_below(xsum)),
            0.25 * (y0 + ym + (yl0 + ylm)),
            0.25 * (zsum + from_below(zsum)),
        ),
        (curl_x, curl_y, curl_z),
        (
            0.5 * (curl_x + curl_x_next),
            0.5 * (curl_y + from_above(curl_y)),
            0.5 * (curl_z + curl_z_next),
        ),
    )


def restrict(
    place, own, x_first, x_second, z_first, z_second, restricted, field, side, planes
):
    fill_masked(place, own, x_first, x_second, z_first, z_second, field, side, planes)
    for layer in range(2):
        for tile in range(HROWS // 8):
            start = 8 * tile
            spaces = restrict_tile(field, side, layer + 1, start, 8)
            for space in range(4):
                for comp in range(3):
                    restricted[space, comp, layer, start : start + 8] = spaces[space][comp]


def band(table, out):
    row = lax.broadcasted_iota(jnp.int32, (8, N), 0)
    lane = lax.broadcasted_iota(jnp.int32, (8, N), 1)

    def codes(at):
        term = (at >= TERM).astype(jnp.int32) + (at >= 2 * TERM).astype(jnp.int32)
        k = at - TERM * term
        dz = (k & 7) - row
        fits = (at < DEPTH) & (row < BLOCK) & (dz >= 0) & (dz < 3)
        return jnp.where(fits, (k >> 3) * 8 + dz, -1)

    code = (codes(lane), codes(lane + N))

    def fill(step, carry):
        space = step // 9
        entry = step % 9
        dy = entry // 3
        d = entry % 3
        rows = []
        for to in range(4):
            halves = [jnp.zeros((8, N), F32), jnp.zeros((8, N), F32)]
            for layer in range(2):
                dx = layer + 2 - to
                if dx < 0 or dx > 2:
                    continue
                for c in range(3):
                    for dz in range(3):
                        index = ((space * 27 + dx * 9 + dy * 3 + dz) * 3 + d) * 3 + c
                        value = table[pl.ds(index, 8, stride=0)]
                        for half in range(2 if c == 2 else 1):
                            hit = code[half] == (c * 2 + layer) * 8 + dz
                            halves[half] = jnp.where(hit, value, halves[half])
            parts = []
            for half, v in enumerate(halves):
                high = v.astype(BF16).astype(F32)
                parts.append(jnp.where(lane + half * N < 2 * TERM, high, v - high))
            rows.append(jnp.concatenate(parts, 1))
        start = pl.multiple_of(entry * 32, 32)
        out[space, pl.ds(start, 32)] = jnp.concatenate(rows, 0).astype(BF16)
        return carry

    lax.fori_loop(0, 36, fill, 0)


def correct(place, restricted, got, weights, out, first, second, w, sent):
    grp = place[0]
    blk = place[1]
    odd = blk % 2

    def dense(space, carry):
        for pair in range(PAIRS):
            starts = (2 * BLOCK * pair, 2 * BLOCK * pair + BLOCK)
            blocks = []
            for at in starts:
                inv = [got[space, layer * INV + at : layer * INV + at + 8] for layer in range(2)]
                blocks.append(jnp.concatenate([
                    restricted[space, c, layer, at : at + 8] * inv[layer]
                    for c in range(3) for layer in range(2)
                ], 0))
            fields = jnp.concatenate(blocks, 1)
            high = fields.astype(BF16)
            low = (fields - high.astype(F32)).astype(BF16)
            sums = jnp.dot(
                weights[space, :, 0:DEPTH],
                jnp.concatenate([high, low, high], 0),
                preferred_element_type=F32,
            )
            for half, at in enumerate(starts):
                lanes = slice(half * N, half * N + N)
                for d in range(3):
                    for to in range(4):
                        below, here, above = (
                            sums[row * 8 : row * 8 + 8, lanes]
                            for row in ((dy * 3 + d) * 4 + to for dy in range(3))
                        )
                        w[space, d, to, at : at + 8] = here + (
                            from_below(below) + from_above(above)
                        )
        return carry

    lax.fori_loop(0, 4, dense, 0)

    def clear(layers, rows):
        for space in range(4):
            for d in range(3):
                for layer in layers:
                    w[space, d, layer, rows] = jnp.zeros((rows.stop - rows.start, N), F32)

    @pl.when(grp == 0)
    def _():
        clear(range(4), slice(0, 1))

    @pl.when(grp == 3)
    def _():
        clear(range(4), slice(N + 1, N + 2))

    @pl.when(blk == 0)
    def _():
        clear((0,), slice(0, WROWS))

    @pl.when(blk == place[2])
    def _():
        clear((3,), slice(0, WROWS))

    for tile in range(N // 8):
        start = 8 * tile
        rows = slice(start, start + 8)

        def at(space, d, layer, shift):
            return w[space, d, layer, start + 1 + shift : start + 9 + shift]

        def along_x(shift):
            half = [0.5 * at(3, 0, layer, shift) for layer in range(4)]
            inner = [at(2, 0, layer, shift) + half[layer] for layer in range(4)]
            return [inner[0]] + [inner[i] + half[i - 1] for i in (1, 2, 3)] + [half[3]]

        def along_y(layer, shift):
            v = at(3, 1, layer, shift)
            return at(2, 1, layer, shift) + 0.5 * (v + from_below(v))

        def along_z(layer):
            return at(2, 2, layer, 0) + 0.5 * (at(3, 2, layer, 0) + at(3, 2, layer, -1))

        tx = along_x(0)
        tx_next = along_x(1)
        ty = [along_y(layer, 0) for layer in range(4)]
        tz = [along_z(layer) for layer in range(4)]
        y_sum = [0.25 * (at(1, 1, layer, 0) + at(1, 1, layer, 1)) for layer in range(4)]
        z_own = [at(1, 2, layer, 0) for layer in range(4)]
        z_sum = [0.25 * (v + from_above(v)) for v in z_own]
        xs, ys, zs = [], [], []
        for layer in range(4):
            x_sum = at(1, 0, layer, 0) + at(1, 0, layer, 1)
            xs.append(
                at(0, 0, layer, 0) + 0.25 * (x_sum + from_above(x_sum))
                + (ty[layer] - along_y(layer, 1)) - (tz[layer] - from_above(tz[layer]))
            )
        for layer in range(-1, 5):
            y = z = None
            if layer >= 0:
                y = tx_next[layer] - tx[layer]
                z = tx[layer] - from_above(tx[layer])
            if 0 <= layer < 4:
                y = y + (at(0, 1, layer, 0) + y_sum[layer] + tz[layer])
                z = z + (at(0, 2, layer, 0) + z_sum[layer] - ty[layer])
            if layer < 3:
                y_more = y_sum[layer + 1] - tz[layer + 1]
                z_more = z_sum[layer + 1] + ty[layer + 1]
                y = y_more if y is None else y + y_more
                z = z_more if z is None else z + z_more
            ys.append(y)
            zs.append(z)
        for layer in range(2):
            out[0, layer, rows] = xs[layer + 1]
            out[1, layer, rows] = ys[layer + 2]
            out[2, layer, rows] = zs[layer + 2]
        up = (xs[3], ys[4], zs[4], ys[5], zs[5])
        down = (xs[0], ys[1], zs[1], ys[0], zs[0])
        for slot in range(5):
            sent[1 - odd, slot, rows] = up[slot]
            sent[odd, slot, rows] = down[slot]
    first[...] = sent[0]
    second[...] = sent[1]


def combine(place, part, first, second, mask, out_hbm, total, out, sems):
    odd = place[1] % 2
    other = 1 - odd
    copies = []
    for comp in range(3):
        at_odd = part[comp, odd] + first[comp]
        at_other = part[comp, other] + second[comp]
        if comp > 0:
            at_odd += second[comp + 2]
            at_other += first[comp + 2]
        total[comp, odd] = at_odd
        total[comp, other] = at_other
        for layer in range(2):
            out[comp, layer] = total[comp, layer].T * mask[comp, layer].astype(F32)
        copies.append(pltpu.make_async_copy(out.at[comp], out_hbm.at[comp], sems.at[comp]))
        copies[-1].start()
    for copy in copies:
        copy.wait()


def correction(residual, face_mask, conductivity, stencil):
    blocks = lax.axis_size("blk")

    def swap(axis, message, begin):
        pairs = [(i, i + 1) for i in range(begin, lax.axis_size(axis) - 1, 2)]
        return lax.ppermute(message, axis, pairs + [(j, i) for i, j in pairs])

    def exchange(axis, first, second):
        return swap(axis, first, 1), swap(axis, second, 0)

    place = jnp.stack(
        [lax.axis_index("grp"), lax.axis_index("blk"), jnp.int32(blocks - 1)]
    ).astype(jnp.int32)

    at = [lax.broadcasted_iota(jnp.int32, stencil.shape, dim) for dim in range(4)]
    diagonal = at[2] == at[3]
    centre = jnp.where(diagonal[:, 13], stencil[:, 13], 0.0)
    step = OMEGA / centre.sum(2)
    twice = jnp.where(diagonal & (at[1] == 13), 2.0, 0.0)
    table = step[:, None, :, None] * (twice - stencil * step[:, None, None, :])
    table = jnp.broadcast_to(table.reshape(972, 1), (972, N))

    in_hbm = pl.BlockSpec(memory_space=pltpu.HBM)
    residual, mask, conductivity = (
        pltpu.with_memory_space_constraint(v, pltpu.HBM)
        for v in (residual, face_mask, conductivity)
    )
    own, first, second, cond = call(
        mask_residual,
        [(3, 2, N, N), (2, N, N), (2, N, N), (1, 2, N, 4 * N)],
        [smem()] + [in_hbm] * 3,
        [
            pltpu.VMEM((3, 2, N, N), F32),
            pltpu.VMEM((3, 2, N, N), jnp.int32),
            pltpu.SemaphoreType.DMA((3,)),
        ],
    )(place, residual, mask, conductivity)
    x_first = swap("blk", first, 1)
    x_second = swap("blk", second, 0)
    (chunks,) = call(invert, [(4, 2 * INV, N)], [vmem()])(cond)
    got = lax.all_to_all(chunks, "grp", split_axis=0, concat_axis=0, tiled=True)
    first, second = call(
        pack, [(PLANES, N), (PLANES, N)], [smem()] + [vmem()] * 3,
        [pltpu.VMEM((2, PLANES, N), F32)],
    )(place, own, x_first, x_second)
    z_first, z_second = exchange("grp", first, second)
    (weights,) = call(band, [(4, 36 * 8, 2 * N)], [vmem()], dtype=BF16)(table)
    (restricted,) = call(
        restrict, [(4, 3, 2, HROWS, N)], [smem()] + [vmem()] * 5,
        [
            pltpu.VMEM((2, 3, MROWS, N), F32),
            pltpu.VMEM((2, 2, MROWS, N), F32),
            pltpu.VMEM((2, PLANES, N), F32),
        ],
    )(place, own, x_first, x_second, z_first, z_second)
    part, first, second = call(
        correct,
        [(3, 2, N, N), (5, N, N), (5, N, N)],
        [smem()] + [vmem()] * 3,
        [
            pltpu.VMEM((4, 3, 4, WROWS, N), F32),
            pltpu.VMEM((2, 5, N, N), F32),
        ],
    )(place, restricted, got, weights)
    first, second = exchange("blk", first, second)
    (out,) = call(
        combine, [(3, 2, N, N)], [smem()] + [vmem()] * 4,
        [
            pltpu.VMEM((3, 2, N, N), F32),
            pltpu.VMEM((3, 2, N, N), F32),
            pltpu.SemaphoreType.DMA((3,)),
        ],
        outs=in_hbm,
    )(place, part, first, second, face_mask)
    return out


def solution(mesh):
    return jax.shard_map(
        correction,
        mesh=mesh,
        in_specs=(
            P(None, "blk", None, "grp"),
            P(None, "blk", None, "grp"),
            P("grp", "blk", None, None),
            P(),
        ),
        out_specs=P(None, "blk", None, "grp"),
        check_vma=False,
    )
```

profile of v0, /device:TPU:6, one launch (start us, length us, event | category | flops | bytes accessed | tf_op | source)
XLA Modules:
  0.0 47.2 jit_solution(4284749235477114224)
XLA Ops:
  0.0 0.1 pad_add_fusion.place
  0.1 1.9 %shard_map.46 = (f32[3,2,128,128]{3,2,1,0:T(8,128)S(1)}, f32[2,128,128]{2,1,0:T(8,128)S(1)}, f32[2,128,128]{2,1,0:T(8,128)S(1)}, f32[1,2,128,512]{3,2,1,0:T(8,128)S(1)}) custom-call(s32[3]{0:T(128)S(1)} %pad_add_fusion.place, f32[3,2,128,128]{3,2,1,0:T(8,128)} %res_hbm.1, s32[3,2,128,128]{3,2,1,0:T(8,128)} %mask.1, f32[1,2,128,512]{3,2,1,0:T(8,128)} %cond_hbm.1), custom_call_target="tpu_custom_call" | custom-call | tf_op jit(solution)/shard_map/pallas_call | solution.py:402
  2.0 8.5 %collective-permute-start = (f32[2,128,128]{2,1,0:T(8,128)S(1)}, f32[2,128,128]{2,1,0:T(8,128)S(1)}, u32[]{:S(2)}, u32[]{:S(2)}) collective-permute-start(f32[2,128,128]{2,1,0:T(8,128)S(1)} %get-tuple-element.15), channel_id=1, source_target_pairs={{1,2},{3,4},{5,6},{7,8},{9,10},{11,12},{13,14},{15,16},{17,18},{19... | collective-permute-start | bytes 393224 | tf_op jit(solution)/shard_map/ppermute | solution.py:380
  10.5 0.1 collective-permute-start.1
  10.6 1.0 %shard_map.49 = f32[4,272,128]{2,1,0:T(8,128)} custom-call(f32[1,2,128,512]{3,2,1,0:T(8,128)S(1)} %get-tuple-element.19.cond), custom_call_target="tpu_custom_call" | custom-call | tf_op jit(solution)/shard_map/pallas_call | solution.py:414
  11.6 3.5 %all-to-all-start = ((f32[4,272,128]{2,1,0:T(8,128)}), f32[4,272,128]{2,1,0:T(8,128)S(1)}, u32[]{:S(2)}, u32[]{:S(2)}) async-start(f32[4,272,128]{2,1,0:T(8,128)} %shard_map.49), calls=%async_computation | async-start | bytes 1114112 | tf_op jit(solution)/shard_map/all_to_all | solution.py:415
  15.1 0.2 select_reduce_fusion
  15.3 0.2 collective-permute-done.1.x_second
  15.5 0.6 %shard_map.47 = (f32[32,128]{1,0:T(8,128)S(1)}, f32[32,128]{1,0:T(8,128)S(1)}) custom-call(s32[3]{0:T(128)S(1)} %pad_add_fusion.place, f32[3,2,128,128]{3,2,1,0:T(8,128)S(1)} %get-tuple-element.14.own, f32[2,128,128]{2,1,0:T(8,128)S(1)} %collective-permute-done.x_first, f32[2,128,128]{2,1,0:T(8,128)S(1)} %collective-permute-done.1.x_second), custom_call_target="tpu_custom_call" | custom-call | tf_op jit(solution)/shard_map/pallas_call | solution.py:416
  16.1 0.7 %collective-permute-start.2 = (f32[32,128]{1,0:T(8,128)S(1)}, f32[32,128]{1,0:T(8,128)S(1)}, u32[]{:S(2)}, u32[]{:S(2)}) collective-permute-start(f32[32,128]{1,0:T(8,128)S(1)} %get-tuple-element.17), channel_id=1, source_target_pairs={{32,64},{64,32},{33,65},{65,33},{34,66},{66,34},{35,67},{67,35},{3... | collective-permute-start | bytes 49160 | tf_op jit(solution)/shard_map/ppermute | solution.py:380
  16.8 3.2 %collective-permute-start.3 = (f32[32,128]{1,0:T(8,128)S(1)}, f32[32,128]{1,0:T(8,128)S(1)}, u32[]{:S(2)}, u32[]{:S(2)}) collective-permute-start(f32[32,128]{1,0:T(8,128)S(1)} %get-tuple-element.18), channel_id=1, source_target_pairs={{0,32},{64,96},{32,0},{96,64},{1,33},{65,97},{33,1},{97,65},{2,34}... | collective-permute-start | bytes 49160 | tf_op jit(solution)/shard_map/ppermute | solution.py:380
  20.0 0.1 subtract_multiply_fusion
  20.0 0.2 copy.5
  20.2 0.2 broadcast_in_dim.24
  20.5 0.2 broadcast_in_dim.25.table
  20.7 1.6 %shard_map.50.weights = bf16[4,288,256]{2,1,0:T(8,128)(2,1)S(1)} custom-call(f32[972,128]{1,0:T(8,128)S(1)} %broadcast_in_dim.25.table), custom_call_target="tpu_custom_call" | custom-call | tf_op jit(solution)/shard_map/pallas_call | solution.py:421
  22.3 0.9 %shard_map.48.restricted = f32[4,3,2,136,128]{4,3,2,1,0:T(8,128)S(1)} custom-call(s32[3]{0:T(128)S(1)} %pad_add_fusion.place, f32[3,2,128,128]{3,2,1,0:T(8,128)S(1)} %get-tuple-element.14.own, f32[2,128,128]{2,1,0:T(8,128)S(1)} %collective-permute-done.x_first, f32[2,128,128]{2,1,0:T(8,128)S(1)} %collective-permute-done.1.x_second, ...), custom_call_target="tpu_custom_call" | custom-call | tf_op jit(solution)/shard_map/pallas_call | solution.py:422
  23.2 0.0 copy-start
  23.3 1.0 %all-to-all-done.got = f32[4,272,128]{2,1,0:T(8,128)S(1)} async-done(((f32[4,272,128]{2,1,0:T(8,128)}), f32[4,272,128]{2,1,0:T(8,128)S(1)}, u32[]{:S(2)}, u32[]{:S(2)}) %all-to-all-start) | async-done | bytes 557088 | tf_op jit(solution)/shard_map/all_to_all | solution.py:415
  24.2 4.6 %shard_map.51 = (f32[3,2,128,128]{3,2,1,0:T(8,128)S(1)}, f32[5,128,128]{2,1,0:T(8,128)S(1)}, f32[5,128,128]{2,1,0:T(8,128)S(1)}) custom-call(s32[3]{0:T(128)S(1)} %pad_add_fusion.place, f32[4,3,2,136,128]{4,3,2,1,0:T(8,128)S(1)} %shard_map.48.restricted, f32[4,272,128]{2,1,0:T(8,128)S(1)} %all-to-all-done.got, bf16[4,288,256]{2,1,0:T(8,128)(2,1)S(1)} %shard_map.50.weights), custom_call_target="tpu_custom_call" | custom-call | tf_op jit(solution)/shard_map/pallas_call | solution.py:430
  28.9 5.5 %collective-permute-start.4 = (f32[5,128,128]{2,1,0:T(8,128)S(1)}, f32[5,128,128]{2,1,0:T(8,128)S(1)}, u32[]{:S(2)}, u32[]{:S(2)}) collective-permute-start(f32[5,128,128]{2,1,0:T(8,128)S(1)} %get-tuple-element.21), channel_id=1, source_target_pairs={{1,2},{3,4},{5,6},{7,8},{9,10},{11,12},{13,14},{15,16},{17,18},{19... | collective-permute-start | bytes 983048 | tf_op jit(solution)/shard_map/ppermute | solution.py:380
  34.4 0.1 collective-permute-start.5
  34.5 11.2 %collective-permute-done.4.first = f32[5,128,128]{2,1,0:T(8,128)S(1)} collective-permute-done((f32[5,128,128]{2,1,0:T(8,128)S(1)}, f32[5,128,128]{2,1,0:T(8,128)S(1)}, u32[]{:S(2)}, u32[]{:S(2)}) %collective-permute-start.4) | collective-permute-done | bytes 327712 | tf_op jit(solution)/shard_map/ppermute | solution.py:380
  45.7 1.5 %shard_map.52 = f32[3,2,128,128]{3,2,1,0:T(8,128)} custom-call(s32[3]{0:T(128)S(1)} %pad_add_fusion.place, f32[3,2,128,128]{3,2,1,0:T(8,128)S(1)} %get-tuple-element.20.part, f32[5,128,128]{2,1,0:T(8,128)S(1)} %collective-permute-done.4.first, f32[5,128,128]{2,1,0:T(8,128)S(1)} %collective-permute-done.5.second, s32[3,2,128,128]{3,2,1,0:T(8,128)S(1)} %copy-done), custom_call_target="tpu_custom_call" | custom-call | tf_op jit(solution)/shard_map/pallas_call | solution.py:440
  (10 shorter events, 0.0 us)
Async XLA Ops:
  0.1 15.0 %copy-start.1 = (f32[4,27,3,3]{1,0,3,2:T(4,128)S(1)}, f32[4,27,3,3]{1,0,3,2:T(4,128)}, u32[]{:S(2)}) copy-start(f32[4,27,3,3]{1,0,3,2:T(4,128)} %param.7) | copy-start | bytes 11668
  2.0 13.3 %collective-permute-start = (f32[2,128,128]{2,1,0:T(8,128)S(1)}, f32[2,128,128]{2,1,0:T(8,128)S(1)}, u32[]{:S(2)}, u32[]{:S(2)}) collective-permute-start(f32[2,128,128]{2,1,0:T(8,128)S(1)} %get-tuple-element.15), channel_id=1, source_target_pairs={{1,2},{3,4},{5,6},{7,8},{9,10},{11,12},{13,14},{15,16},{17,18},{19... | collective-permute-start | bytes 393224 | tf_op jit(solution)/shard_map/ppermute | solution.py:380
  10.5 5.0 %collective-permute-start.1 = (f32[2,128,128]{2,1,0:T(8,128)S(1)}, f32[2,128,128]{2,1,0:T(8,128)S(1)}, u32[]{:S(2)}, u32[]{:S(2)}) collective-permute-start(f32[2,128,128]{2,1,0:T(8,128)S(1)} %get-tuple-element.16), channel_id=1, source_target_pairs={{0,1},{2,3},{4,5},{6,7},{8,9},{10,11},{12,13},{14,15},{16,17},{18,... | collective-permute-start | bytes 393224 | tf_op jit(solution)/shard_map/ppermute | solution.py:380
  11.6 12.6 %all-to-all-start = ((f32[4,272,128]{2,1,0:T(8,128)}), f32[4,272,128]{2,1,0:T(8,128)S(1)}, u32[]{:S(2)}, u32[]{:S(2)}) async-start(f32[4,272,128]{2,1,0:T(8,128)} %shard_map.49), calls=%async_computation | async-start | bytes 1114112 | tf_op jit(solution)/shard_map/all_to_all | solution.py:415
  16.1 6.2 %collective-permute-start.2 = (f32[32,128]{1,0:T(8,128)S(1)}, f32[32,128]{1,0:T(8,128)S(1)}, u32[]{:S(2)}, u32[]{:S(2)}) collective-permute-start(f32[32,128]{1,0:T(8,128)S(1)} %get-tuple-element.17), channel_id=1, source_target_pairs={{32,64},{64,32},{33,65},{65,33},{34,66},{66,34},{35,67},{67,35},{3... | collective-permute-start | bytes 49160 | tf_op jit(solution)/shard_map/ppermute | solution.py:380
  16.8 5.5 %collective-permute-start.3 = (f32[32,128]{1,0:T(8,128)S(1)}, f32[32,128]{1,0:T(8,128)S(1)}, u32[]{:S(2)}, u32[]{:S(2)}) collective-permute-start(f32[32,128]{1,0:T(8,128)S(1)} %get-tuple-element.18), channel_id=1, source_target_pairs={{0,32},{64,96},{32,0},{96,64},{1,33},{65,97},{33,1},{97,65},{2,34}... | collective-permute-start | bytes 49160 | tf_op jit(solution)/shard_map/ppermute | solution.py:380
  23.2 22.5 %copy-start = (s32[3,2,128,128]{3,2,1,0:T(8,128)S(1)}, s32[3,2,128,128]{3,2,1,0:T(8,128)}, u32[]{:S(2)}) copy-start(s32[3,2,128,128]{3,2,1,0:T(8,128)} %mask.1) | copy-start | bytes 1179652
  28.9 16.9 %collective-permute-start.4 = (f32[5,128,128]{2,1,0:T(8,128)S(1)}, f32[5,128,128]{2,1,0:T(8,128)S(1)}, u32[]{:S(2)}, u32[]{:S(2)}) collective-permute-start(f32[5,128,128]{2,1,0:T(8,128)S(1)} %get-tuple-element.21), channel_id=1, source_target_pairs={{1,2},{3,4},{5,6},{7,8},{9,10},{11,12},{13,14},{15,16},{17,18},{19... | collective-permute-start | bytes 983048 | tf_op jit(solution)/shard_map/ppermute | solution.py:380
  34.4 11.3 %collective-permute-start.5 = (f32[5,128,128]{2,1,0:T(8,128)S(1)}, f32[5,128,128]{2,1,0:T(8,128)S(1)}, u32[]{:S(2)}, u32[]{:S(2)}) collective-permute-start(f32[5,128,128]{2,1,0:T(8,128)S(1)} %get-tuple-element.22), channel_id=1, source_target_pairs={{0,1},{2,3},{4,5},{6,7},{8,9},{10,11},{12,13},{14,15},{16,17},{18,... | collective-permute-start | bytes 983048 | tf_op jit(solution)/shard_map/ppermute | solution.py:380
where the time goes:
time: 47.7 us; the launch traced here: 47.2 us
  starting transfers between devices  21.5 us (45%)
  waiting for transfers between devices  12.5 us (26%)
  Pallas kernels  12.2 us (26%)
  local copies, waits for them, and re-layouts  0.61 us (1%)
    ppermute x6, starting transfers between devices, swap(): return lax.ppermute(message, axis, pairs + [(j, i) for i, j in pairs])  18 us
    ppermute x6, waiting for transfers between devices, swap(): return lax.ppermute(message, axis, pairs + [(j, i) for i, j in pairs])  11.5 us
    pallas_call x1, Pallas kernels, correction(): call(correct, [(3, 2, N, N), (5, N, N), (5, N, N)], [smem()] + [vmem()] *...  4.64 us
    all_to_all x1, starting transfers between devices, correction(): got = lax.all_to_all(chunks, 'grp', split_axis=0, concat_axis=0, tiled=True)  3.47 us
    pallas_call x1, Pallas kernels, correction(): call(mask_residual, [(3, 2, N, N), (2, N, N), (2, N, N), (1, 2, N, 4 * N)...  1.9 us
    pallas_call x1, Pallas kernels, correction(): weights, = call(band, [(4, 36 * 8, 2 * N)], [vmem()], dtype=BF16)(table)  1.6 us
    pallas_call x1, Pallas kernels, correction(): call(combine, [(3, 2, N, N)], [smem()] + [vmem()] * 4, [pltpu.VMEM((3, 2,...  1.48 us
    pallas_call x1, Pallas kernels, correction(): chunks, = call(invert, [(4, 2 * INV, N)], [vmem()])(cond)  1.02 us
  transfers between devices with their start and end apart: 7, of which 3 were waited for; matrix products, arithmetic and copies ran while one was open for 2% of the time, Pallas kernels for 9%

commit v1 on v0

--- a/solution.py
+++ b/solution.py
@@ -50,7 +50,7 @@
 
 
 def mask_residual(
-    place, res_hbm, mask_hbm, cond_hbm, own, first, second, cond, res, mask, sems
+    place, res_hbm, mask_hbm, cond_hbm, own, first, second, chunks, cond, res, mask, sems
 ):
     odd = place[1] % 2
     copies = [
@@ -68,6 +68,7 @@
         first[slot] = own[slot + 1, odd]
         second[slot] = own[slot + 1, 1 - odd]
     copies[2].wait()
+    invert(cond, chunks)
 
 
 def invert(cond, chunks):
@@ -91,7 +92,7 @@
     return 18 + ((comp - 1) * 2 + max(layer, 0) // 2) * 3
 
 
-def pack(place, own, x_first, x_second, first, second, planes):
+def pack(place, own, x_first, x_second, weights, first, second, planes):
     z_odd = place[0] % 2
     odd = place[1] % 2
 
@@ -228,7 +229,7 @@
         out[space, pl.ds(start, 32)] = jnp.concatenate(rows, 0).astype(BF16)
         return carry
 
-    lax.fori_loop(0, 36, fill, 0)
+    lax.fori_loop(0, 36, fill, 0, unroll=3)
 
 
 def correct(place, restricted, got, weights, out, first, second, w, sent):
@@ -267,7 +268,7 @@
                         )
         return carry
 
-    lax.fori_loop(0, 4, dense, 0)
+    lax.fori_loop(0, 4, dense, 0, unroll=4)
 
     def clear(layers, rows):
         for space in range(4):
@@ -399,11 +400,12 @@
         pltpu.with_memory_space_constraint(v, pltpu.HBM)
         for v in (residual, face_mask, conductivity)
     )
-    own, first, second, cond = call(
+    own, first, second, chunks = call(
         mask_residual,
-        [(3, 2, N, N), (2, N, N), (2, N, N), (1, 2, N, 4 * N)],
+        [(3, 2, N, N), (2, N, N), (2, N, N), (4, 2 * INV, N)],
         [smem()] + [in_hbm] * 3,
         [
+            pltpu.VMEM((1, 2, N, 4 * N), F32),
             pltpu.VMEM((3, 2, N, N), F32),
             pltpu.VMEM((3, 2, N, N), jnp.int32),
             pltpu.SemaphoreType.DMA((3,)),
@@ -411,14 +413,14 @@
     )(place, residual, mask, conductivity)
     x_first = swap("blk", first, 1)
     x_second = swap("blk", second, 0)
-    (chunks,) = call(invert, [(4, 2 * INV, N)], [vmem()])(cond)
     got = lax.all_to_all(chunks, "grp", split_axis=0, concat_axis=0, tiled=True)
+    (weights,) = call(band, [(4, 36 * 8, 2 * N)], [vmem()], dtype=BF16)(table)
     first, second = call(
-        pack, [(PLANES, N), (PLANES, N)], [smem()] + [vmem()] * 3,
+        pack, [(PLANES, N), (PLANES, N)],
+        [smem()] + [vmem()] * 3 + [pl.BlockSpec(memory_space=pl.ANY)],
         [pltpu.VMEM((2, PLANES, N), F32)],
-    )(place, own, x_first, x_second)
+    )(place, own, x_first, x_second, weights)
     z_first, z_second = exchange("grp", first, second)
-    (weights,) = call(band, [(4, 36 * 8, 2 * N)], [vmem()], dtype=BF16)(table)
     (restricted,) = call(
         restrict, [(4, 3, 2, HROWS, N)], [smem()] + [vmem()] * 5,
         [

time: 47.7 us -> 48.8 us (1.023)
  waiting for transfers between devices: 12.5 us -> 14.2 us
  Pallas kernels: 12.2 us -> 10.8 us
  starting transfers between devices: 21.5 us -> 22.5 us
    ppermute x6, waiting for transfers between devices: 11.5 us -> 14.2 us  [swap(): return lax.ppermute(message, axis, pairs + [(j, i) for i, j in pairs])]
    ppermute x6, starting transfers between devices: 18 us -> 19 us  [swap(): return lax.ppermute(message, axis, pairs + [(j, i) for i, j in pairs])]
    all_to_all x1, waiting for transfers between devices: 0.96 us -> 0.01 us  [correction(): got = lax.all_to_all(chunks, 'grp', split_axis=0, concat_axis=0, tiled=True)]
    pallas_call x1, Pallas kernels: 4.64 us -> 3.78 us  [correction(): call(correct, [(3, 2, N, N), (5, N, N), (5, N, N)], [smem()] + [vmem()] *...]
    pallas_call x1, Pallas kernels: 1.6 us -> 1.07 us  [correction(): weights, = call(band, [(4, 36 * 8, 2 * N)], [vmem()], dtype=BF16)(table)]
    pallas_call x3 -> x2, Pallas kernels: 3.48 us -> 3.48 us  [the longest x1 2.92 us: correction(): call(mask_residual, [(3, 2, N, N), (2, N, N), (2, N, N), (4, 2 * INV, N)]...]
  transfers between devices with their start and end apart: 7 -> 7, of which waited for: 3 -> 5; matrix products, arithmetic and copies ran while one was open for 2% -> 2% of each run, Pallas kernels for 9% -> 5%
where the time goes in v1:
time: 48.8 us; the launch traced here: 48.6 us
  starting transfers between devices  22.5 us (46%)
  waiting for transfers between devices  14.2 us (29%)
  Pallas kernels  10.8 us (22%)
  local copies, waits for them, and re-layouts  0.62 us (1%)
    ppermute x6, starting transfers between devices, swap(): return lax.ppermute(message, axis, pairs + [(j, i) for i, j in pairs])  19 us
    ppermute x6, waiting for transfers between devices, swap(): return lax.ppermute(message, axis, pairs + [(j, i) for i, j in pairs])  14.2 us
    pallas_call x1, Pallas kernels, correction(): call(correct, [(3, 2, N, N), (5, N, N), (5, N, N)], [smem()] + [vmem()] *...  3.78 us
    all_to_all x1, starting transfers between devices, correction(): got = lax.all_to_all(chunks, 'grp', split_axis=0, concat_axis=0, tiled=True)  3.48 us
    pallas_call x1, Pallas kernels, correction(): call(mask_residual, [(3, 2, N, N), (2, N, N), (2, N, N), (4, 2 * INV, N)]...  2.92 us
    pallas_call x1, Pallas kernels, correction(): call(combine, [(3, 2, N, N)], [smem()] + [vmem()] * 4, [pltpu.VMEM((3, 2,...  1.48 us
    pallas_call x1, Pallas kernels, correction(): weights, = call(band, [(4, 36 * 8, 2 * N)], [vmem()], dtype=BF16)(table)  1.07 us
  transfers between devices with their start and end apart: 7, of which 5 were waited for; matrix products, arithmetic and copies ran while one was open for 2% of the time, Pallas kernels for 5%

profile of v1, /device:TPU:6, one launch (start us, length us, event | category | flops | bytes accessed | tf_op | source)
XLA Modules:
  0.0 48.6 jit_solution(1757988829596883971)
XLA Ops:
  0.0 0.1 pad_add_fusion.place
  0.1 2.9 %shard_map.46 = (f32[3,2,128,128]{3,2,1,0:T(8,128)S(1)}, f32[2,128,128]{2,1,0:T(8,128)S(1)}, f32[2,128,128]{2,1,0:T(8,128)S(1)}, f32[4,272,128]{2,1,0:T(8,128)}) custom-call(s32[3]{0:T(128)S(1)} %pad_add_fusion.place, f32[3,2,128,128]{3,2,1,0:T(8,128)} %res_hbm.1, s32[3,2,128,128]{3,2,1,0:T(8,128)} %mask.1, f32[1,2,128,512]{3,2,1,0:T(8,128)} %cond_hbm.1), custom_call_target="tpu_custom_call" | custom-call | tf_op jit(solution)/shard_map/pallas_call | solution.py:403
  3.0 3.5 %all-to-all-start = ((f32[4,272,128]{2,1,0:T(8,128)}), f32[4,272,128]{2,1,0:T(8,128)S(1)}, u32[]{:S(2)}, u32[]{:S(2)}) async-start(f32[4,272,128]{2,1,0:T(8,128)} %get-tuple-element.19), calls=%async_computation | async-start | bytes 1114112 | tf_op jit(solution)/shard_map/all_to_all | solution.py:416
  6.5 8.5 %collective-permute-start = (f32[2,128,128]{2,1,0:T(8,128)S(1)}, f32[2,128,128]{2,1,0:T(8,128)S(1)}, u32[]{:S(2)}, u32[]{:S(2)}) collective-permute-start(f32[2,128,128]{2,1,0:T(8,128)S(1)} %get-tuple-element.15), channel_id=1, source_target_pairs={{1,2},{3,4},{5,6},{7,8},{9,10},{11,12},{13,14},{15,16},{17,18},{19... | collective-permute-start | bytes 393224 | tf_op jit(solution)/shard_map/ppermute | solution.py:381
  15.0 0.1 collective-permute-start.1
  15.1 0.2 select_reduce_fusion
  15.3 0.1 subtract_multiply_fusion
  15.4 0.2 copy.5
  15.6 0.2 broadcast_in_dim.24
  15.8 0.2 broadcast_in_dim.25.table
  16.0 1.1 %shard_map.47.weights = bf16[4,288,256]{2,1,0:T(8,128)(2,1)S(1)} custom-call(f32[972,128]{1,0:T(8,128)S(1)} %broadcast_in_dim.25.table), custom_call_target="tpu_custom_call" | custom-call | tf_op jit(solution)/shard_map/pallas_call | solution.py:417
  17.1 2.1 %collective-permute-done.x_first = f32[2,128,128]{2,1,0:T(8,128)S(1)} collective-permute-done((f32[2,128,128]{2,1,0:T(8,128)S(1)}, f32[2,128,128]{2,1,0:T(8,128)S(1)}, u32[]{:S(2)}, u32[]{:S(2)}) %collective-permute-start) | collective-permute-done | bytes 131104 | tf_op jit(solution)/shard_map/ppermute | solution.py:381
  19.2 1.5 %collective-permute-done.1.x_second = f32[2,128,128]{2,1,0:T(8,128)S(1)} collective-permute-done((f32[2,128,128]{2,1,0:T(8,128)S(1)}, f32[2,128,128]{2,1,0:T(8,128)S(1)}, u32[]{:S(2)}, u32[]{:S(2)}) %collective-permute-start.1) | collective-permute-done | bytes 131104 | tf_op jit(solution)/shard_map/ppermute | solution.py:381
  20.7 0.6 %shard_map.48 = (f32[32,128]{1,0:T(8,128)S(1)}, f32[32,128]{1,0:T(8,128)S(1)}) custom-call(s32[3]{0:T(128)S(1)} %pad_add_fusion.place, f32[3,2,128,128]{3,2,1,0:T(8,128)S(1)} %get-tuple-element.14.own, f32[2,128,128]{2,1,0:T(8,128)S(1)} %collective-permute-done.x_first, f32[2,128,128]{2,1,0:T(8,128)S(1)} %collective-permute-done.1.x_second, ...), custom_call_target="tpu_custom_call" | custom-call | tf_op jit(solution)/shard_map/pallas_call | solution.py:418
  21.2 0.7 %collective-permute-start.2 = (f32[32,128]{1,0:T(8,128)S(1)}, f32[32,128]{1,0:T(8,128)S(1)}, u32[]{:S(2)}, u32[]{:S(2)}) collective-permute-start(f32[32,128]{1,0:T(8,128)S(1)} %get-tuple-element.17), channel_id=1, source_target_pairs={{32,64},{64,32},{33,65},{65,33},{34,66},{66,34},{35,67},{67,35},{3... | collective-permute-start | bytes 49160 | tf_op jit(solution)/shard_map/ppermute | solution.py:381
  21.9 2.5 %collective-permute-start.3 = (f32[32,128]{1,0:T(8,128)S(1)}, f32[32,128]{1,0:T(8,128)S(1)}, u32[]{:S(2)}, u32[]{:S(2)}) collective-permute-start(f32[32,128]{1,0:T(8,128)S(1)} %get-tuple-element.18), channel_id=1, source_target_pairs={{0,32},{64,96},{32,0},{96,64},{1,33},{65,97},{33,1},{97,65},{2,34}... | collective-permute-start | bytes 49160 | tf_op jit(solution)/shard_map/ppermute | solution.py:381
  24.4 0.8 %collective-permute-done.3.z_second = f32[32,128]{1,0:T(8,128)S(1)} collective-permute-done((f32[32,128]{1,0:T(8,128)S(1)}, f32[32,128]{1,0:T(8,128)S(1)}, u32[]{:S(2)}, u32[]{:S(2)}) %collective-permute-start.3) | collective-permute-done | bytes 16416 | tf_op jit(solution)/shard_map/ppermute | solution.py:381
  25.2 0.9 %shard_map.49.restricted = f32[4,3,2,136,128]{4,3,2,1,0:T(8,128)S(1)} custom-call(s32[3]{0:T(128)S(1)} %pad_add_fusion.place, f32[3,2,128,128]{3,2,1,0:T(8,128)S(1)} %get-tuple-element.14.own, f32[2,128,128]{2,1,0:T(8,128)S(1)} %collective-permute-done.x_first, f32[2,128,128]{2,1,0:T(8,128)S(1)} %collective-permute-done.1.x_second, ...), custom_call_target="tpu_custom_call" | custom-call | tf_op jit(solution)/shard_map/pallas_call | solution.py:424
  26.2 3.8 %shard_map.50 = (f32[3,2,128,128]{3,2,1,0:T(8,128)S(1)}, f32[5,128,128]{2,1,0:T(8,128)S(1)}, f32[5,128,128]{2,1,0:T(8,128)S(1)}) custom-call(s32[3]{0:T(128)S(1)} %pad_add_fusion.place, f32[4,3,2,136,128]{4,3,2,1,0:T(8,128)S(1)} %shard_map.49.restricted, f32[4,272,128]{2,1,0:T(8,128)S(1)} %all-to-all-done.got, bf16[4,288,256]{2,1,0:T(8,128)(2,1)S(1)} %shard_map.47.weights), custom_call_target="tpu_custom_call" | custom-call | tf_op jit(solution)/shard_map/pallas_call | solution.py:432
  30.0 7.2 %collective-permute-start.4 = (f32[5,128,128]{2,1,0:T(8,128)S(1)}, f32[5,128,128]{2,1,0:T(8,128)S(1)}, u32[]{:S(2)}, u32[]{:S(2)}) collective-permute-start(f32[5,128,128]{2,1,0:T(8,128)S(1)} %get-tuple-element.21), channel_id=1, source_target_pairs={{1,2},{3,4},{5,6},{7,8},{9,10},{11,12},{13,14},{15,16},{17,18},{19... | collective-permute-start | bytes 983048 | tf_op jit(solution)/shard_map/ppermute | solution.py:381
  37.2 0.1 collective-permute-start.5
  37.3 9.2 %collective-permute-done.4.first = f32[5,128,128]{2,1,0:T(8,128)S(1)} collective-permute-done((f32[5,128,128]{2,1,0:T(8,128)S(1)}, f32[5,128,128]{2,1,0:T(8,128)S(1)}, u32[]{:S(2)}, u32[]{:S(2)}) %collective-permute-start.4) | collective-permute-done | bytes 327712 | tf_op jit(solution)/shard_map/ppermute | solution.py:381
  46.5 0.6 %collective-permute-done.5.second = f32[5,128,128]{2,1,0:T(8,128)S(1)} collective-permute-done((f32[5,128,128]{2,1,0:T(8,128)S(1)}, f32[5,128,128]{2,1,0:T(8,128)S(1)}, u32[]{:S(2)}, u32[]{:S(2)}) %collective-permute-start.5) | collective-permute-done | bytes 327712 | tf_op jit(solution)/shard_map/ppermute | solution.py:381
  47.1 1.5 %shard_map.51 = f32[3,2,128,128]{3,2,1,0:T(8,128)} custom-call(s32[3]{0:T(128)S(1)} %pad_add_fusion.place, f32[3,2,128,128]{3,2,1,0:T(8,128)S(1)} %get-tuple-element.20.part, f32[5,128,128]{2,1,0:T(8,128)S(1)} %collective-permute-done.4.first, f32[5,128,128]{2,1,0:T(8,128)S(1)} %collective-permute-done.5.second, s32[3,2,128,128]{3,2,1,0:T(8,128)S(1)} %copy-done), custom_call_target="tpu_custom_call" | custom-call | tf_op jit(solution)/shard_map/pallas_call | solution.py:442
  (9 shorter events, 0.0 us)
Async XLA Ops:
  0.0 15.1 %copy-start.1 = (f32[4,27,3,3]{1,0,3,2:T(4,128)S(1)}, f32[4,27,3,3]{1,0,3,2:T(4,128)}, u32[]{:S(2)}) copy-start(f32[4,27,3,3]{1,0,3,2:T(4,128)} %param.7) | copy-start | bytes 11668
  3.0 23.2 %all-to-all-start = ((f32[4,272,128]{2,1,0:T(8,128)}), f32[4,272,128]{2,1,0:T(8,128)S(1)}, u32[]{:S(2)}, u32[]{:S(2)}) async-start(f32[4,272,128]{2,1,0:T(8,128)} %get-tuple-element.19), calls=%async_computation | async-start | bytes 1114112 | tf_op jit(solution)/shard_map/all_to_all | solution.py:416
  6.5 12.7 %collective-permute-start = (f32[2,128,128]{2,1,0:T(8,128)S(1)}, f32[2,128,128]{2,1,0:T(8,128)S(1)}, u32[]{:S(2)}, u32[]{:S(2)}) collective-permute-start(f32[2,128,128]{2,1,0:T(8,128)S(1)} %get-tuple-element.15), channel_id=1, source_target_pairs={{1,2},{3,4},{5,6},{7,8},{9,10},{11,12},{13,14},{15,16},{17,18},{19... | collective-permute-start | bytes 393224 | tf_op jit(solution)/shard_map/ppermute | solution.py:381
  15.0 5.7 %collective-permute-start.1 = (f32[2,128,128]{2,1,0:T(8,128)S(1)}, f32[2,128,128]{2,1,0:T(8,128)S(1)}, u32[]{:S(2)}, u32[]{:S(2)}) collective-permute-start(f32[2,128,128]{2,1,0:T(8,128)S(1)} %get-tuple-element.16), channel_id=1, source_target_pairs={{0,1},{2,3},{4,5},{6,7},{8,9},{10,11},{12,13},{14,15},{16,17},{18,... | collective-permute-start | bytes 393224 | tf_op jit(solution)/shard_map/ppermute | solution.py:381
  21.2 3.1 %collective-permute-start.2 = (f32[32,128]{1,0:T(8,128)S(1)}, f32[32,128]{1,0:T(8,128)S(1)}, u32[]{:S(2)}, u32[]{:S(2)}) collective-permute-start(f32[32,128]{1,0:T(8,128)S(1)} %get-tuple-element.17), channel_id=1, source_target_pairs={{32,64},{64,32},{33,65},{65,33},{34,66},{66,34},{35,67},{67,35},{3... | collective-permute-start | bytes 49160 | tf_op jit(solution)/shard_map/ppermute | solution.py:381
  21.9 3.3 %collective-permute-start.3 = (f32[32,128]{1,0:T(8,128)S(1)}, f32[32,128]{1,0:T(8,128)S(1)}, u32[]{:S(2)}, u32[]{:S(2)}) collective-permute-start(f32[32,128]{1,0:T(8,128)S(1)} %get-tuple-element.18), channel_id=1, source_target_pairs={{0,32},{64,96},{32,0},{96,64},{1,33},{65,97},{33,1},{97,65},{2,34}... | collective-permute-start | bytes 49160 | tf_op jit(solution)/shard_map/ppermute | solution.py:381
  26.2 20.9 %copy-start = (s32[3,2,128,128]{3,2,1,0:T(8,128)S(1)}, s32[3,2,128,128]{3,2,1,0:T(8,128)}, u32[]{:S(2)}) copy-start(s32[3,2,128,128]{3,2,1,0:T(8,128)} %mask.1) | copy-start | bytes 1179652
  30.0 16.5 %collective-permute-start.4 = (f32[5,128,128]{2,1,0:T(8,128)S(1)}, f32[5,128,128]{2,1,0:T(8,128)S(1)}, u32[]{:S(2)}, u32[]{:S(2)}) collective-permute-start(f32[5,128,128]{2,1,0:T(8,128)S(1)} %get-tuple-element.21), channel_id=1, source_target_pairs={{1,2},{3,4},{5,6},{7,8},{9,10},{11,12},{13,14},{15,16},{17,18},{19... | collective-permute-start | bytes 983048 | tf_op jit(solution)/shard_map/ppermute | solution.py:381
  37.2 9.9 %collective-permute-start.5 = (f32[5,128,128]{2,1,0:T(8,128)S(1)}, f32[5,128,128]{2,1,0:T(8,128)S(1)}, u32[]{:S(2)}, u32[]{:S(2)}) collective-permute-start(f32[5,128,128]{2,1,0:T(8,128)S(1)} %get-tuple-element.22), channel_id=1, source_target_pairs={{0,1},{2,3},{4,5},{6,7},{8,9},{10,11},{12,13},{14,15},{16,17},{18,... | collective-permute-start | bytes 983048 | tf_op jit(solution)/shard_map/ppermute | solution.py:381

commit v2 on v1

--- a/solution.py
+++ b/solution.py
@@ -33,7 +33,7 @@
         kernel,
         out_shape=[jax.ShapeDtypeStruct(shape, dtype) for shape in out_shapes],
         in_specs=in_specs,
-        out_specs=[outs or vmem() for _ in out_shapes],
+        out_specs=outs or [vmem() for _ in out_shapes],
         scratch_shapes=list(scratch),
         compiler_params=pltpu.CompilerParams(vmem_limit_bytes=50 << 20),
     )
@@ -50,7 +50,8 @@
 
 
 def mask_residual(
-    place, res_hbm, mask_hbm, cond_hbm, own, first, second, chunks, cond, res, mask, sems
+    place, res_hbm, mask_hbm, cond_hbm, own, first, second, chunks_hbm,
+    chunks, cond, res, mask, sems,
 ):
     odd = place[1] % 2
     copies = [
@@ -59,6 +60,10 @@
     ]
     for copy in copies:
         copy.start()
+    copies[2].wait()
+    invert(cond, chunks)
+    leave = pltpu.make_async_copy(chunks, chunks_hbm, sems.at[3])
+    leave.start()
     copies[0].wait()
     copies[1].wait()
     for comp in range(3):
@@ -67,8 +72,7 @@
     for slot in range(2):
         first[slot] = own[slot + 1, odd]
         second[slot] = own[slot + 1, 1 - odd]
-    copies[2].wait()
-    invert(cond, chunks)
+    leave.wait()
 
 
 def invert(cond, chunks):
@@ -405,11 +409,13 @@
         [(3, 2, N, N), (2, N, N), (2, N, N), (4, 2 * INV, N)],
         [smem()] + [in_hbm] * 3,
         [
+            pltpu.VMEM((4, 2 * INV, N), F32),
             pltpu.VMEM((1, 2, N, 4 * N), F32),
             pltpu.VMEM((3, 2, N, N), F32),
             pltpu.VMEM((3, 2, N, N), jnp.int32),
-            pltpu.SemaphoreType.DMA((3,)),
+            pltpu.SemaphoreType.DMA((4,)),
         ],
+        outs=[vmem()] * 3 + [in_hbm],
     )(place, residual, mask, conductivity)
     x_first = swap("blk", first, 1)
     x_second = swap("blk", second, 0)
@@ -446,7 +452,7 @@
             pltpu.VMEM((3, 2, N, N), F32),
             pltpu.SemaphoreType.DMA((3,)),
         ],
-        outs=in_hbm,
+        outs=[in_hbm],
     )(place, part, first, second, face_mask)
     return out
 

time: 48.8 us -> 48.8 us (level)
  no operation moved by 1% of the time
where the time goes in v2:
time: 48.8 us; the launch traced here: 48.5 us
  starting transfers between devices  22.5 us (46%)
  waiting for transfers between devices  14.2 us (29%)
  Pallas kernels  10.7 us (22%)
  local copies, waits for them, and re-layouts  0.62 us (1%)
    ppermute x6, starting transfers between devices, swap(): return lax.ppermute(message, axis, pairs + [(j, i) for i, j in pairs])  19 us
    ppermute x6, waiting for transfers between devices, swap(): return lax.ppermute(message, axis, pairs + [(j, i) for i, j in pairs])  14.2 us
    pallas_call x1, Pallas kernels, correction(): call(correct, [(3, 2, N, N), (5, N, N), (5, N, N)], [smem()] + [vmem()] *...  3.78 us
    all_to_all x1, starting transfers between devices, correction(): got = lax.all_to_all(chunks, 'grp', split_axis=0, concat_axis=0, tiled=True)  3.48 us
    pallas_call x1, Pallas kernels, correction(): call(mask_residual, [(3, 2, N, N), (2, N, N), (2, N, N), (4, 2 * INV, N)]...  2.87 us
    pallas_call x1, Pallas kernels, correction(): call(combine, [(3, 2, N, N)], [smem()] + [vmem()] * 4, [pltpu.VMEM((3, 2,...  1.48 us
    pallas_call x1, Pallas kernels, correction(): weights, = call(band, [(4, 36 * 8, 2 * N)], [vmem()], dtype=BF16)(table)  1.07 us
  transfers between devices with their start and end apart: 7, of which 5 were waited for; matrix products, arithmetic and copies ran while one was open for 2% of the time, Pallas kernels for 5%

profile of v2, /device:TPU:6, one launch (start us, length us, event | category | flops | bytes accessed | tf_op | source)
XLA Modules:
  0.0 48.5 jit_solution(5714115499317794392)
XLA Ops:
  0.0 0.1 pad_add_fusion.place
  0.1 2.9 %shard_map.46 = (f32[3,2,128,128]{3,2,1,0:T(8,128)S(1)}, f32[2,128,128]{2,1,0:T(8,128)S(1)}, f32[2,128,128]{2,1,0:T(8,128)S(1)}, f32[4,272,128]{2,1,0:T(8,128)}) custom-call(s32[3]{0:T(128)S(1)} %pad_add_fusion.place, f32[3,2,128,128]{3,2,1,0:T(8,128)} %res_hbm.1, s32[3,2,128,128]{3,2,1,0:T(8,128)} %mask.1, f32[1,2,128,512]{3,2,1,0:T(8,128)} %cond_hbm.1), custom_call_target="tpu_custom_call" | custom-call | tf_op jit(solution)/shard_map/pallas_call | solution.py:407
  3.0 3.5 %all-to-all-start = ((f32[4,272,128]{2,1,0:T(8,128)}), f32[4,272,128]{2,1,0:T(8,128)S(1)}, u32[]{:S(2)}, u32[]{:S(2)}) async-start(f32[4,272,128]{2,1,0:T(8,128)} %get-tuple-element.19), calls=%async_computation | async-start | bytes 1114112 | tf_op jit(solution)/shard_map/all_to_all | solution.py:422
  6.5 8.5 %collective-permute-start = (f32[2,128,128]{2,1,0:T(8,128)S(1)}, f32[2,128,128]{2,1,0:T(8,128)S(1)}, u32[]{:S(2)}, u32[]{:S(2)}) collective-permute-start(f32[2,128,128]{2,1,0:T(8,128)S(1)} %get-tuple-element.15), channel_id=1, source_target_pairs={{1,2},{3,4},{5,6},{7,8},{9,10},{11,12},{13,14},{15,16},{17,18},{19... | collective-permute-start | bytes 393224 | tf_op jit(solution)/shard_map/ppermute | solution.py:385
  15.0 0.1 collective-permute-start.1
  15.1 0.2 select_reduce_fusion
  15.3 0.1 subtract_multiply_fusion
  15.3 0.2 copy.5
  15.6 0.2 broadcast_in_dim.24
  15.8 0.2 broadcast_in_dim.25.table
  16.0 1.1 %shard_map.47.weights = bf16[4,288,256]{2,1,0:T(8,128)(2,1)S(1)} custom-call(f32[972,128]{1,0:T(8,128)S(1)} %broadcast_in_dim.25.table), custom_call_target="tpu_custom_call" | custom-call | tf_op jit(solution)/shard_map/pallas_call | solution.py:423
  17.0 2.1 %collective-permute-done.x_first = f32[2,128,128]{2,1,0:T(8,128)S(1)} collective-permute-done((f32[2,128,128]{2,1,0:T(8,128)S(1)}, f32[2,128,128]{2,1,0:T(8,128)S(1)}, u32[]{:S(2)}, u32[]{:S(2)}) %collective-permute-start) | collective-permute-done | bytes 131104 | tf_op jit(solution)/shard_map/ppermute | solution.py:385
  19.2 1.5 %collective-permute-done.1.x_second = f32[2,128,128]{2,1,0:T(8,128)S(1)} collective-permute-done((f32[2,128,128]{2,1,0:T(8,128)S(1)}, f32[2,128,128]{2,1,0:T(8,128)S(1)}, u32[]{:S(2)}, u32[]{:S(2)}) %collective-permute-start.1) | collective-permute-done | bytes 131104 | tf_op jit(solution)/shard_map/ppermute | solution.py:385
  20.6 0.6 %shard_map.48 = (f32[32,128]{1,0:T(8,128)S(1)}, f32[32,128]{1,0:T(8,128)S(1)}) custom-call(s32[3]{0:T(128)S(1)} %pad_add_fusion.place, f32[3,2,128,128]{3,2,1,0:T(8,128)S(1)} %get-tuple-element.14.own, f32[2,128,128]{2,1,0:T(8,128)S(1)} %collective-permute-done.x_first, f32[2,128,128]{2,1,0:T(8,128)S(1)} %collective-permute-done.1.x_second, ...), custom_call_target="tpu_custom_call" | custom-call | tf_op jit(solution)/shard_map/pallas_call | solution.py:424
  21.2 0.7 %collective-permute-start.2 = (f32[32,128]{1,0:T(8,128)S(1)}, f32[32,128]{1,0:T(8,128)S(1)}, u32[]{:S(2)}, u32[]{:S(2)}) collective-permute-start(f32[32,128]{1,0:T(8,128)S(1)} %get-tuple-element.17), channel_id=1, source_target_pairs={{32,64},{64,32},{33,65},{65,33},{34,66},{66,34},{35,67},{67,35},{3... | collective-permute-start | bytes 49160 | tf_op jit(solution)/shard_map/ppermute | solution.py:385
  21.9 2.5 %collective-permute-start.3 = (f32[32,128]{1,0:T(8,128)S(1)}, f32[32,128]{1,0:T(8,128)S(1)}, u32[]{:S(2)}, u32[]{:S(2)}) collective-permute-start(f32[32,128]{1,0:T(8,128)S(1)} %get-tuple-element.18), channel_id=1, source_target_pairs={{0,32},{64,96},{32,0},{96,64},{1,33},{65,97},{33,1},{97,65},{2,34}... | collective-permute-start | bytes 49160 | tf_op jit(solution)/shard_map/ppermute | solution.py:385
  24.3 0.8 %collective-permute-done.3.z_second = f32[32,128]{1,0:T(8,128)S(1)} collective-permute-done((f32[32,128]{1,0:T(8,128)S(1)}, f32[32,128]{1,0:T(8,128)S(1)}, u32[]{:S(2)}, u32[]{:S(2)}) %collective-permute-start.3) | collective-permute-done | bytes 16416 | tf_op jit(solution)/shard_map/ppermute | solution.py:385
  25.2 0.9 %shard_map.49.restricted = f32[4,3,2,136,128]{4,3,2,1,0:T(8,128)S(1)} custom-call(s32[3]{0:T(128)S(1)} %pad_add_fusion.place, f32[3,2,128,128]{3,2,1,0:T(8,128)S(1)} %get-tuple-element.14.own, f32[2,128,128]{2,1,0:T(8,128)S(1)} %collective-permute-done.x_first, f32[2,128,128]{2,1,0:T(8,128)S(1)} %collective-permute-done.1.x_second, ...), custom_call_target="tpu_custom_call" | custom-call | tf_op jit(solution)/shard_map/pallas_call | solution.py:430
  26.1 3.8 %shard_map.50 = (f32[3,2,128,128]{3,2,1,0:T(8,128)S(1)}, f32[5,128,128]{2,1,0:T(8,128)S(1)}, f32[5,128,128]{2,1,0:T(8,128)S(1)}) custom-call(s32[3]{0:T(128)S(1)} %pad_add_fusion.place, f32[4,3,2,136,128]{4,3,2,1,0:T(8,128)S(1)} %shard_map.49.restricted, f32[4,272,128]{2,1,0:T(8,128)S(1)} %all-to-all-done.got, bf16[4,288,256]{2,1,0:T(8,128)(2,1)S(1)} %shard_map.47.weights), custom_call_target="tpu_custom_call" | custom-call | tf_op jit(solution)/shard_map/pallas_call | solution.py:438
  29.9 7.2 %collective-permute-start.4 = (f32[5,128,128]{2,1,0:T(8,128)S(1)}, f32[5,128,128]{2,1,0:T(8,128)S(1)}, u32[]{:S(2)}, u32[]{:S(2)}) collective-permute-start(f32[5,128,128]{2,1,0:T(8,128)S(1)} %get-tuple-element.21), channel_id=1, source_target_pairs={{1,2},{3,4},{5,6},{7,8},{9,10},{11,12},{13,14},{15,16},{17,18},{19... | collective-permute-start | bytes 983048 | tf_op jit(solution)/shard_map/ppermute | solution.py:385
  37.1 0.1 collective-permute-start.5
  37.2 9.2 %collective-permute-done.4.first = f32[5,128,128]{2,1,0:T(8,128)S(1)} collective-permute-done((f32[5,128,128]{2,1,0:T(8,128)S(1)}, f32[5,128,128]{2,1,0:T(8,128)S(1)}, u32[]{:S(2)}, u32[]{:S(2)}) %collective-permute-start.4) | collective-permute-done | bytes 327712 | tf_op jit(solution)/shard_map/ppermute | solution.py:385
  46.4 0.6 %collective-permute-done.5.second = f32[5,128,128]{2,1,0:T(8,128)S(1)} collective-permute-done((f32[5,128,128]{2,1,0:T(8,128)S(1)}, f32[5,128,128]{2,1,0:T(8,128)S(1)}, u32[]{:S(2)}, u32[]{:S(2)}) %collective-permute-start.5) | collective-permute-done | bytes 327712 | tf_op jit(solution)/shard_map/ppermute | solution.py:385
  47.1 1.5 %shard_map.51 = f32[3,2,128,128]{3,2,1,0:T(8,128)} custom-call(s32[3]{0:T(128)S(1)} %pad_add_fusion.place, f32[3,2,128,128]{3,2,1,0:T(8,128)S(1)} %get-tuple-element.20.part, f32[5,128,128]{2,1,0:T(8,128)S(1)} %collective-permute-done.4.first, f32[5,128,128]{2,1,0:T(8,128)S(1)} %collective-permute-done.5.second, s32[3,2,128,128]{3,2,1,0:T(8,128)S(1)} %copy-done), custom_call_target="tpu_custom_call" | custom-call | tf_op jit(solution)/shard_map/pallas_call | solution.py:448
  (9 shorter events, 0.0 us)
Async XLA Ops:
  0.0 15.1 %copy-start.1 = (f32[4,27,3,3]{1,0,3,2:T(4,128)S(1)}, f32[4,27,3,3]{1,0,3,2:T(4,128)}, u32[]{:S(2)}) copy-start(f32[4,27,3,3]{1,0,3,2:T(4,128)} %param.7) | copy-start | bytes 11668
  3.0 23.2 %all-to-all-start = ((f32[4,272,128]{2,1,0:T(8,128)}), f32[4,272,128]{2,1,0:T(8,128)S(1)}, u32[]{:S(2)}, u32[]{:S(2)}) async-start(f32[4,272,128]{2,1,0:T(8,128)} %get-tuple-element.19), calls=%async_computation | async-start | bytes 1114112 | tf_op jit(solution)/shard_map/all_to_all | solution.py:422
  6.5 12.7 %collective-permute-start = (f32[2,128,128]{2,1,0:T(8,128)S(1)}, f32[2,128,128]{2,1,0:T(8,128)S(1)}, u32[]{:S(2)}, u32[]{:S(2)}) collective-permute-start(f32[2,128,128]{2,1,0:T(8,128)S(1)} %get-tuple-element.15), channel_id=1, source_target_pairs={{1,2},{3,4},{5,6},{7,8},{9,10},{11,12},{13,14},{15,16},{17,18},{19... | collective-permute-start | bytes 393224 | tf_op jit(solution)/shard_map/ppermute | solution.py:385
  15.0 5.7 %collective-permute-start.1 = (f32[2,128,128]{2,1,0:T(8,128)S(1)}, f32[2,128,128]{2,1,0:T(8,128)S(1)}, u32[]{:S(2)}, u32[]{:S(2)}) collective-permute-start(f32[2,128,128]{2,1,0:T(8,128)S(1)} %get-tuple-element.16), channel_id=1, source_target_pairs={{0,1},{2,3},{4,5},{6,7},{8,9},{10,11},{12,13},{14,15},{16,17},{18,... | collective-permute-start | bytes 393224 | tf_op jit(solution)/shard_map/ppermute | solution.py:385
  21.2 3.1 %collective-permute-start.2 = (f32[32,128]{1,0:T(8,128)S(1)}, f32[32,128]{1,0:T(8,128)S(1)}, u32[]{:S(2)}, u32[]{:S(2)}) collective-permute-start(f32[32,128]{1,0:T(8,128)S(1)} %get-tuple-element.17), channel_id=1, source_target_pairs={{32,64},{64,32},{33,65},{65,33},{34,66},{66,34},{35,67},{67,35},{3... | collective-permute-start | bytes 49160 | tf_op jit(solution)/shard_map/ppermute | solution.py:385
  21.9 3.3 %collective-permute-start.3 = (f32[32,128]{1,0:T(8,128)S(1)}, f32[32,128]{1,0:T(8,128)S(1)}, u32[]{:S(2)}, u32[]{:S(2)}) collective-permute-start(f32[32,128]{1,0:T(8,128)S(1)} %get-tuple-element.18), channel_id=1, source_target_pairs={{0,32},{64,96},{32,0},{96,64},{1,33},{65,97},{33,1},{97,65},{2,34}... | collective-permute-start | bytes 49160 | tf_op jit(solution)/shard_map/ppermute | solution.py:385
  26.1 20.9 %copy-start = (s32[3,2,128,128]{3,2,1,0:T(8,128)S(1)}, s32[3,2,128,128]{3,2,1,0:T(8,128)}, u32[]{:S(2)}) copy-start(s32[3,2,128,128]{3,2,1,0:T(8,128)} %mask.1) | copy-start | bytes 1179652
  29.9 16.5 %collective-permute-start.4 = (f32[5,128,128]{2,1,0:T(8,128)S(1)}, f32[5,128,128]{2,1,0:T(8,128)S(1)}, u32[]{:S(2)}, u32[]{:S(2)}) collective-permute-start(f32[5,128,128]{2,1,0:T(8,128)S(1)} %get-tuple-element.21), channel_id=1, source_target_pairs={{1,2},{3,4},{5,6},{7,8},{9,10},{11,12},{13,14},{15,16},{17,18},{19... | collective-permute-start | bytes 983048 | tf_op jit(solution)/shard_map/ppermute | solution.py:385
  37.1 9.9 %collective-permute-start.5 = (f32[5,128,128]{2,1,0:T(8,128)S(1)}, f32[5,128,128]{2,1,0:T(8,128)S(1)}, u32[]{:S(2)}, u32[]{:S(2)}) collective-permute-start(f32[5,128,128]{2,1,0:T(8,128)S(1)} %get-tuple-element.22), channel_id=1, source_target_pairs={{0,1},{2,3},{4,5},{6,7},{8,9},{10,11},{12,13},{14,15},{16,17},{18,... | collective-permute-start | bytes 983048 | tf_op jit(solution)/shard_map/ppermute | solution.py:385

commit v3 on v2

--- a/solution.py
+++ b/solution.py
@@ -371,8 +371,10 @@
         total[comp, other] = at_other
         for layer in range(2):
             out[comp, layer] = total[comp, layer].T * mask[comp, layer].astype(F32)
-        copies.append(pltpu.make_async_copy(out.at[comp], out_hbm.at[comp], sems.at[comp]))
-        copies[-1].start()
+            copies.append(pltpu.make_async_copy(
+                out.at[comp, layer], out_hbm.at[comp, layer], sems.at[2 * comp + layer]
+            ))
+            copies[-1].start()
     for copy in copies:
         copy.wait()
 
@@ -450,7 +452,7 @@
         [
             pltpu.VMEM((3, 2, N, N), F32),
             pltpu.VMEM((3, 2, N, N), F32),
-            pltpu.SemaphoreType.DMA((3,)),
+            pltpu.SemaphoreType.DMA((6,)),
         ],
         outs=[in_hbm],
     )(place, part, first, second, face_mask)

time: 48.8 us -> 48.8 us (level)
  no operation moved by 1% of the time
where the time goes in v3:
time: 48.8 us; the launch traced here: 48.6 us
  starting transfers between devices  22.5 us (46%)
  waiting for transfers between devices  14.2 us (29%)
  Pallas kernels  10.7 us (22%)
  local copies, waits for them, and re-layouts  0.62 us (1%)
    ppermute x6, starting transfers between devices, swap(): return lax.ppermute(message, axis, pairs + [(j, i) for i, j in pairs])  19 us
    ppermute x6, waiting for transfers between devices, swap(): return lax.ppermute(message, axis, pairs + [(j, i) for i, j in pairs])  14.2 us
    pallas_call x1, Pallas kernels, correction(): call(correct, [(3, 2, N, N), (5, N, N), (5, N, N)], [smem()] + [vmem()] *...  3.78 us
    all_to_all x1, starting transfers between devices, correction(): got = lax.all_to_all(chunks, 'grp', split_axis=0, concat_axis=0, tiled=True)  3.48 us
    pallas_call x1, Pallas kernels, correction(): call(mask_residual, [(3, 2, N, N), (2, N, N), (2, N, N), (4, 2 * INV, N)]...  2.87 us
    pallas_call x1, Pallas kernels, correction(): call(combine, [(3, 2, N, N)], [smem()] + [vmem()] * 4, [pltpu.VMEM((3, 2,...  1.51 us
    pallas_call x1, Pallas kernels, correction(): weights, = call(band, [(4, 36 * 8, 2 * N)], [vmem()], dtype=BF16)(table)  1.07 us
  transfers between devices with their start and end apart: 7, of which 5 were waited for; matrix products, arithmetic and copies ran while one was open for 2% of the time, Pallas kernels for 5%

profile of v3, /device:TPU:6, one launch (start us, length us, event | category | flops | bytes accessed | tf_op | source)
XLA Modules:
  0.0 48.6 jit_solution(13579854840103739940)
XLA Ops:
  0.0 0.1 pad_add_fusion.place
  0.1 2.9 %shard_map.46 = (f32[3,2,128,128]{3,2,1,0:T(8,128)S(1)}, f32[2,128,128]{2,1,0:T(8,128)S(1)}, f32[2,128,128]{2,1,0:T(8,128)S(1)}, f32[4,272,128]{2,1,0:T(8,128)}) custom-call(s32[3]{0:T(128)S(1)} %pad_add_fusion.place, f32[3,2,128,128]{3,2,1,0:T(8,128)} %res_hbm.1, s32[3,2,128,128]{3,2,1,0:T(8,128)} %mask.1, f32[1,2,128,512]{3,2,1,0:T(8,128)} %cond_hbm.1), custom_call_target="tpu_custom_call" | custom-call | tf_op jit(solution)/shard_map/pallas_call | solution.py:409
  3.0 3.5 %all-to-all-start = ((f32[4,272,128]{2,1,0:T(8,128)}), f32[4,272,128]{2,1,0:T(8,128)S(1)}, u32[]{:S(2)}, u32[]{:S(2)}) async-start(f32[4,272,128]{2,1,0:T(8,128)} %get-tuple-element.19), calls=%async_computation | async-start | bytes 1114112 | tf_op jit(solution)/shard_map/all_to_all | solution.py:424
  6.5 8.5 %collective-permute-start = (f32[2,128,128]{2,1,0:T(8,128)S(1)}, f32[2,128,128]{2,1,0:T(8,128)S(1)}, u32[]{:S(2)}, u32[]{:S(2)}) collective-permute-start(f32[2,128,128]{2,1,0:T(8,128)S(1)} %get-tuple-element.15), channel_id=1, source_target_pairs={{1,2},{3,4},{5,6},{7,8},{9,10},{11,12},{13,14},{15,16},{17,18},{19... | collective-permute-start | bytes 393224 | tf_op jit(solution)/shard_map/ppermute | solution.py:387
  15.0 0.1 collective-permute-start.1
  15.1 0.2 select_reduce_fusion
  15.3 0.1 subtract_multiply_fusion
  15.3 0.2 copy.5
  15.6 0.2 broadcast_in_dim.24
  15.8 0.2 broadcast_in_dim.25.table
  16.0 1.1 %shard_map.47.weights = bf16[4,288,256]{2,1,0:T(8,128)(2,1)S(1)} custom-call(f32[972,128]{1,0:T(8,128)S(1)} %broadcast_in_dim.25.table), custom_call_target="tpu_custom_call" | custom-call | tf_op jit(solution)/shard_map/pallas_call | solution.py:425
  17.0 2.1 %collective-permute-done.x_first = f32[2,128,128]{2,1,0:T(8,128)S(1)} collective-permute-done((f32[2,128,128]{2,1,0:T(8,128)S(1)}, f32[2,128,128]{2,1,0:T(8,128)S(1)}, u32[]{:S(2)}, u32[]{:S(2)}) %collective-permute-start) | collective-permute-done | bytes 131104 | tf_op jit(solution)/shard_map/ppermute | solution.py:387
  19.2 1.5 %collective-permute-done.1.x_second = f32[2,128,128]{2,1,0:T(8,128)S(1)} collective-permute-done((f32[2,128,128]{2,1,0:T(8,128)S(1)}, f32[2,128,128]{2,1,0:T(8,128)S(1)}, u32[]{:S(2)}, u32[]{:S(2)}) %collective-permute-start.1) | collective-permute-done | bytes 131104 | tf_op jit(solution)/shard_map/ppermute | solution.py:387
  20.6 0.6 %shard_map.48 = (f32[32,128]{1,0:T(8,128)S(1)}, f32[32,128]{1,0:T(8,128)S(1)}) custom-call(s32[3]{0:T(128)S(1)} %pad_add_fusion.place, f32[3,2,128,128]{3,2,1,0:T(8,128)S(1)} %get-tuple-element.14.own, f32[2,128,128]{2,1,0:T(8,128)S(1)} %collective-permute-done.x_first, f32[2,128,128]{2,1,0:T(8,128)S(1)} %collective-permute-done.1.x_second, ...), custom_call_target="tpu_custom_call" | custom-call | tf_op jit(solution)/shard_map/pallas_call | solution.py:426
  21.2 0.7 %collective-permute-start.2 = (f32[32,128]{1,0:T(8,128)S(1)}, f32[32,128]{1,0:T(8,128)S(1)}, u32[]{:S(2)}, u32[]{:S(2)}) collective-permute-start(f32[32,128]{1,0:T(8,128)S(1)} %get-tuple-element.17), channel_id=1, source_target_pairs={{32,64},{64,32},{33,65},{65,33},{34,66},{66,34},{35,67},{67,35},{3... | collective-permute-start | bytes 49160 | tf_op jit(solution)/shard_map/ppermute | solution.py:387
  21.9 2.5 %collective-permute-start.3 = (f32[32,128]{1,0:T(8,128)S(1)}, f32[32,128]{1,0:T(8,128)S(1)}, u32[]{:S(2)}, u32[]{:S(2)}) collective-permute-start(f32[32,128]{1,0:T(8,128)S(1)} %get-tuple-element.18), channel_id=1, source_target_pairs={{0,32},{64,96},{32,0},{96,64},{1,33},{65,97},{33,1},{97,65},{2,34}... | collective-permute-start | bytes 49160 | tf_op jit(solution)/shard_map/ppermute | solution.py:387
  24.3 0.8 %collective-permute-done.3.z_second = f32[32,128]{1,0:T(8,128)S(1)} collective-permute-done((f32[32,128]{1,0:T(8,128)S(1)}, f32[32,128]{1,0:T(8,128)S(1)}, u32[]{:S(2)}, u32[]{:S(2)}) %collective-permute-start.3) | collective-permute-done | bytes 16416 | tf_op jit(solution)/shard_map/ppermute | solution.py:387
  25.2 0.9 %shard_map.49.restricted = f32[4,3,2,136,128]{4,3,2,1,0:T(8,128)S(1)} custom-call(s32[3]{0:T(128)S(1)} %pad_add_fusion.place, f32[3,2,128,128]{3,2,1,0:T(8,128)S(1)} %get-tuple-element.14.own, f32[2,128,128]{2,1,0:T(8,128)S(1)} %collective-permute-done.x_first, f32[2,128,128]{2,1,0:T(8,128)S(1)} %collective-permute-done.1.x_second, ...), custom_call_target="tpu_custom_call" | custom-call | tf_op jit(solution)/shard_map/pallas_call | solution.py:432
  26.1 3.8 %shard_map.50 = (f32[3,2,128,128]{3,2,1,0:T(8,128)S(1)}, f32[5,128,128]{2,1,0:T(8,128)S(1)}, f32[5,128,128]{2,1,0:T(8,128)S(1)}) custom-call(s32[3]{0:T(128)S(1)} %pad_add_fusion.place, f32[4,3,2,136,128]{4,3,2,1,0:T(8,128)S(1)} %shard_map.49.restricted, f32[4,272,128]{2,1,0:T(8,128)S(1)} %all-to-all-done.got, bf16[4,288,256]{2,1,0:T(8,128)(2,1)S(1)} %shard_map.47.weights), custom_call_target="tpu_custom_call" | custom-call | tf_op jit(solution)/shard_map/pallas_call | solution.py:440
  29.9 7.2 %collective-permute-start.4 = (f32[5,128,128]{2,1,0:T(8,128)S(1)}, f32[5,128,128]{2,1,0:T(8,128)S(1)}, u32[]{:S(2)}, u32[]{:S(2)}) collective-permute-start(f32[5,128,128]{2,1,0:T(8,128)S(1)} %get-tuple-element.21), channel_id=1, source_target_pairs={{1,2},{3,4},{5,6},{7,8},{9,10},{11,12},{13,14},{15,16},{17,18},{19... | collective-permute-start | bytes 983048 | tf_op jit(solution)/shard_map/ppermute | solution.py:387
  37.1 0.1 collective-permute-start.5
  37.2 9.2 %collective-permute-done.4.first = f32[5,128,128]{2,1,0:T(8,128)S(1)} collective-permute-done((f32[5,128,128]{2,1,0:T(8,128)S(1)}, f32[5,128,128]{2,1,0:T(8,128)S(1)}, u32[]{:S(2)}, u32[]{:S(2)}) %collective-permute-start.4) | collective-permute-done | bytes 327712 | tf_op jit(solution)/shard_map/ppermute | solution.py:387
  46.4 0.6 %collective-permute-done.5.second = f32[5,128,128]{2,1,0:T(8,128)S(1)} collective-permute-done((f32[5,128,128]{2,1,0:T(8,128)S(1)}, f32[5,128,128]{2,1,0:T(8,128)S(1)}, u32[]{:S(2)}, u32[]{:S(2)}) %collective-permute-start.5) | collective-permute-done | bytes 327712 | tf_op jit(solution)/shard_map/ppermute | solution.py:387
  47.1 1.5 %shard_map.51 = f32[3,2,128,128]{3,2,1,0:T(8,128)} custom-call(s32[3]{0:T(128)S(1)} %pad_add_fusion.place, f32[3,2,128,128]{3,2,1,0:T(8,128)S(1)} %get-tuple-element.20.part, f32[5,128,128]{2,1,0:T(8,128)S(1)} %collective-permute-done.4.first, f32[5,128,128]{2,1,0:T(8,128)S(1)} %collective-permute-done.5.second, s32[3,2,128,128]{3,2,1,0:T(8,128)S(1)} %copy-done), custom_call_target="tpu_custom_call" | custom-call | tf_op jit(solution)/shard_map/pallas_call | solution.py:450
  (9 shorter events, 0.0 us)
Async XLA Ops:
  0.0 15.1 %copy-start.1 = (f32[4,27,3,3]{1,0,3,2:T(4,128)S(1)}, f32[4,27,3,3]{1,0,3,2:T(4,128)}, u32[]{:S(2)}) copy-start(f32[4,27,3,3]{1,0,3,2:T(4,128)} %param.7) | copy-start | bytes 11668
  3.0 23.2 %all-to-all-start = ((f32[4,272,128]{2,1,0:T(8,128)}), f32[4,272,128]{2,1,0:T(8,128)S(1)}, u32[]{:S(2)}, u32[]{:S(2)}) async-start(f32[4,272,128]{2,1,0:T(8,128)} %get-tuple-element.19), calls=%async_computation | async-start | bytes 1114112 | tf_op jit(solution)/shard_map/all_to_all | solution.py:424
  6.5 12.7 %collective-permute-start = (f32[2,128,128]{2,1,0:T(8,128)S(1)}, f32[2,128,128]{2,1,0:T(8,128)S(1)}, u32[]{:S(2)}, u32[]{:S(2)}) collective-permute-start(f32[2,128,128]{2,1,0:T(8,128)S(1)} %get-tuple-element.15), channel_id=1, source_target_pairs={{1,2},{3,4},{5,6},{7,8},{9,10},{11,12},{13,14},{15,16},{17,18},{19... | collective-permute-start | bytes 393224 | tf_op jit(solution)/shard_map/ppermute | solution.py:387
  15.0 5.7 %collective-permute-start.1 = (f32[2,128,128]{2,1,0:T(8,128)S(1)}, f32[2,128,128]{2,1,0:T(8,128)S(1)}, u32[]{:S(2)}, u32[]{:S(2)}) collective-permute-start(f32[2,128,128]{2,1,0:T(8,128)S(1)} %get-tuple-element.16), channel_id=1, source_target_pairs={{0,1},{2,3},{4,5},{6,7},{8,9},{10,11},{12,13},{14,15},{16,17},{18,... | collective-permute-start | bytes 393224 | tf_op jit(solution)/shard_map/ppermute | solution.py:387
  21.2 3.1 %collective-permute-start.2 = (f32[32,128]{1,0:T(8,128)S(1)}, f32[32,128]{1,0:T(8,128)S(1)}, u32[]{:S(2)}, u32[]{:S(2)}) collective-permute-start(f32[32,128]{1,0:T(8,128)S(1)} %get-tuple-element.17), channel_id=1, source_target_pairs={{32,64},{64,32},{33,65},{65,33},{34,66},{66,34},{35,67},{67,35},{3... | collective-permute-start | bytes 49160 | tf_op jit(solution)/shard_map/ppermute | solution.py:387
  21.9 3.3 %collective-permute-start.3 = (f32[32,128]{1,0:T(8,128)S(1)}, f32[32,128]{1,0:T(8,128)S(1)}, u32[]{:S(2)}, u32[]{:S(2)}) collective-permute-start(f32[32,128]{1,0:T(8,128)S(1)} %get-tuple-element.18), channel_id=1, source_target_pairs={{0,32},{64,96},{32,0},{96,64},{1,33},{65,97},{33,1},{97,65},{2,34}... | collective-permute-start | bytes 49160 | tf_op jit(solution)/shard_map/ppermute | solution.py:387
  26.1 20.9 %copy-start = (s32[3,2,128,128]{3,2,1,0:T(8,128)S(1)}, s32[3,2,128,128]{3,2,1,0:T(8,128)}, u32[]{:S(2)}) copy-start(s32[3,2,128,128]{3,2,1,0:T(8,128)} %mask.1) | copy-start | bytes 1179652
  29.9 16.5 %collective-permute-start.4 = (f32[5,128,128]{2,1,0:T(8,128)S(1)}, f32[5,128,128]{2,1,0:T(8,128)S(1)}, u32[]{:S(2)}, u32[]{:S(2)}) collective-permute-start(f32[5,128,128]{2,1,0:T(8,128)S(1)} %get-tuple-element.21), channel_id=1, source_target_pairs={{1,2},{3,4},{5,6},{7,8},{9,10},{11,12},{13,14},{15,16},{17,18},{19... | collective-permute-start | bytes 983048 | tf_op jit(solution)/shard_map/ppermute | solution.py:387
  37.1 9.9 %collective-permute-start.5 = (f32[5,128,128]{2,1,0:T(8,128)S(1)}, f32[5,128,128]{2,1,0:T(8,128)S(1)}, u32[]{:S(2)}, u32[]{:S(2)}) collective-permute-start(f32[5,128,128]{2,1,0:T(8,128)S(1)} %get-tuple-element.22), channel_id=1, source_target_pairs={{0,1},{2,3},{4,5},{6,7},{8,9},{10,11},{12,13},{14,15},{16,17},{18,... | collective-permute-start | bytes 983048 | tf_op jit(solution)/shard_map/ppermute | solution.py:387
